TPU v7x, 32 devices: a whole 2x2x4 slice. The times are simulated.
32 devices in a mesh: gx: 2 (over x), gy: 4 (over z), gz: 4 (over y, core).
Axes of the slice: x: 2, y: 2, z: 4, core: 2. Of those that a mesh axis runs over, the one named last changes fastest.
Arguments:
- right_side: float32 [16, 64, 512], P('gx', 'gy', 'gz'), may hold values from -40 to 40
- fiber_class: int32 [16, 64, 512], P('gx', 'gy', 'gz'), may hold values from 0 to 15
- conductivity_scale: float32 [16, 64, 512], P('gx', 'gy', 'gz'), may hold values from 0.8 to 1.25
- class_tensor: float32 [6, 16], replicated, may hold values from -0.15 to 1.8, as said below
- block_ids: int32 [2, 4, 8], replicated, may hold values from 0 to 63, as said below
Outputs:
- solution: float32 [16, 64, 512], P('gx', 'gy', 'gz')
- residual: float32 [16, 64, 512], P('gx', 'gy', 'gz')
Inputs may be any that keep to these rules, and one draw needn't show every extreme that they name: `class_tensor`: column k is the tensor t I + (l - t) f f^T for a unit vector f, with 1 <= t <= 1.5 and 1.05 <= l / t <= 1.2. `block_ids`: each subdomain number names exactly 1 block.
All inputs are finite; a program needn't handle non-finite values.
Results may differ from a plain program's by a relative error of at most 0.0003.
Values sent between devices are 32-bit elements; how exact they have to be, the bound alone decides.
A program may use at most 64 MiB of HBM per device.

v0:
```python
import jax
import jax.numpy as jnp
from jax import lax
from jax.sharding import PartitionSpec as P

CX = 8
CY = 16
CZ = 128
ZBLK = 2
BZ = 64
COARSE = 64
NCLS = 16
ITERS = 2
STENCIL_TAPS = (
    (1, 0, 0, 0, 1.0),
    (-1, 0, 0, 0, 1.0),
    (0, 1, 0, 1, 1.0),
    (0, -1, 0, 1, 1.0),
    (0, 0, 1, 2, 1.0),
    (0, 0, -1, 2, 1.0),
    (1, 1, 0, 3, 0.5),
    (-1, -1, 0, 3, 0.5),
    (1, -1, 0, 3, -0.5),
    (-1, 1, 0, 3, -0.5),
    (1, 0, 1, 4, 0.5),
    (-1, 0, -1, 4, 0.5),
    (1, 0, -1, 4, -0.5),
    (-1, 0, 1, 4, -0.5),
    (0, 1, 1, 5, 0.5),
    (0, -1, -1, 5, 0.5),
    (0, 1, -1, 5, -0.5),
    (0, -1, 1, 5, -0.5),
)


def padded_2(cells, sides, width):
    for axis, dim in sides:
        count = lax.axis_size(axis)
        ends = count - 1
        head = lax.slice_in_dim(cells, 0, width, axis=dim)
        tail = lax.slice_in_dim(cells, cells.shape[dim] - width, cells.shape[dim], axis=dim)
        cells = jnp.concatenate(
            [
                lax.ppermute(tail, axis, [(i, (i + 1) % count) for i in range(ends)]),
                cells,
                lax.ppermute(head, axis, [((i + 1) % count, i) for i in range(ends)]),
            ],
            axis=dim,
        )
    return cells


def shifted(padded, step_x, step_y, step_z):
    width_x = padded.shape[-3] - 2
    width_y = padded.shape[-2] - 2
    width_z = padded.shape[-1] - 2
    return padded[
        1 + step_x : 1 + step_x + width_x,
        1 + step_y : 1 + step_y + width_y,
        1 + step_z : 1 + step_z + width_z,
    ]


def edge_weights(tensors, step_x, step_y, step_z, component, factor):
    layer = tensors[component]
    return 0.5 * factor * (shifted(layer, 0, 0, 0) + shifted(layer, step_x, step_y, step_z))


def operate(padded, tensors):
    centre = shifted(padded, 0, 0, 0)
    accumulated = jnp.zeros_like(centre)
    for step_x, step_y, step_z, component, factor in STENCIL_TAPS:
        weight = edge_weights(tensors, step_x, step_y, step_z, component, factor)
        accumulated = accumulated + weight * (centre - shifted(padded, step_x, step_y, step_z))
    return accumulated


def class_onehot(labels, count):
    return (labels[..., None] == jnp.arange(count, dtype=jnp.int32)).astype(jnp.float32)


def reach_onehot(length, offset):
    position = jnp.arange(length, dtype=jnp.int32)
    relative = (position + offset) // length + 1
    return (relative[:, None] == jnp.arange(3, dtype=jnp.int32)[None, :]).astype(jnp.float32)


def reach_blocks(length, offset, blocks):
    block_span = length // blocks
    position = jnp.arange(length, dtype=jnp.int32)
    owning = (position // block_span)[:, None] == jnp.arange(blocks, dtype=jnp.int32)[None, :]
    relative = ((position % block_span + offset) // block_span + 1)[:, None] == jnp.arange(
        3, dtype=jnp.int32
    )[None, :]
    return (owning[:, :, None] & relative[:, None, :]).astype(jnp.float32)


def centre_mask():
    places = jnp.arange(3, dtype=jnp.int32)
    return (
        (places[:, None, None] == 1) & (places[None, :, None] == 1) & (places[None, None, :] == 1)
    )


def build_tensors(matches, scale, class_tensor):
    return (
        jnp.stack(
            [
                jnp.sum(
                    jnp.where(matches, class_tensor[component][:, None, None, None], 0.0), axis=0
                )
                for component in range(6)
            ]
        )
        * scale[None]
    )


def body(right_side, fiber_class, conductivity_scale, class_tensor, block_ids):
    highest = lax.Precision.HIGHEST
    kinds = jnp.arange(NCLS, dtype=jnp.int32)
    matches = fiber_class[None] == kinds[:, None, None, None]
    local_tensor = build_tensors(matches, conductivity_scale, class_tensor)
    tensors = padded_2(local_tensor, (("gx", 1), ("gy", 2), ("gz", 3)), 1)
    place_x = lax.axis_index("gx")
    place_y = lax.axis_index("gy")
    place_z = lax.axis_index("gz")
    padded_ids = jnp.pad(block_ids, 1, constant_values=-1)
    window = lax.dynamic_slice(padded_ids, (place_x, place_y, place_z * ZBLK), (3, 3, ZBLK + 2))
    own_hot = class_onehot(window[1, 1, 1 : ZBLK + 1], COARSE)
    neighbours = jnp.stack([window[:, :, z_block : z_block + 3] for z_block in range(ZBLK)])
    rim_weight = jnp.zeros((ZBLK, 3, 3, 3), jnp.float32)
    for step_x, step_y, step_z, component, factor in STENCIL_TAPS:
        weight = edge_weights(tensors, step_x, step_y, step_z, component, factor)
        rim_weight = rim_weight + jnp.einsum(
            "xyz,xa,yb,zjc->jabc",
            weight,
            reach_onehot(CX, step_x),
            reach_onehot(CY, step_y),
            reach_blocks(CZ, step_z, ZBLK),
            precision=highest,
        )
    rim_weight = jnp.where(centre_mask()[None], 0.0, rim_weight)
    diagonal_terms = jnp.einsum(
        "jk,j->k", own_hot, jnp.sum(rim_weight, axis=(1, 2, 3)), precision=highest
    )
    coupling = jnp.einsum(
        "jk,jabc,jabcl->kl",
        own_hot,
        rim_weight,
        class_onehot(neighbours, COARSE),
        precision=highest,
    )
    coarse = lax.psum(jnp.diag(diagonal_terms) - coupling, ("gx", "gy", "gz"))
    coarse = 0.5 * (coarse + coarse.T)
    factor_lower = jnp.linalg.cholesky(coarse)

    def restrict(field):
        block_totals = jnp.sum(field.reshape(CX, CY, ZBLK, BZ), axis=(0, 1, 3))
        return jnp.einsum("jk,j->k", own_hot, block_totals, precision=highest)

    def prolong(coarse_values):
        values = jnp.einsum("jk,k->j", own_hot, coarse_values, precision=highest)
        return jnp.broadcast_to(values[None, None, :, None], (CX, CY, ZBLK, BZ)).reshape(CX, CY, CZ)

    def apply_field(field):
        padded = padded_2(field, (("gx", 0), ("gy", 1), ("gz", 2)), 1)
        return operate(padded, tensors)

    def coarse_solve(field):
        projected = lax.psum(restrict(field), ("gx", "gy", "gz"))
        return jax.scipy.linalg.cho_solve((factor_lower, True), projected)

    def deflation_image(coarse_values):
        result = apply_field(prolong(coarse_values))
        return result

    coarse_values = coarse_solve(right_side)
    coarse_part = prolong(coarse_values)
    residual = right_side - deflation_image(coarse_values)
    estimate = jnp.zeros_like(right_side)

    def joint_terms(field):
        product = apply_field(field)
        projected, norm_value, cross_value = lax.psum(
            (restrict(product), jnp.sum(field * field), jnp.sum(field * product)),
            ("gx", "gy", "gz"),
        )
        correction = jax.scipy.linalg.cho_solve((factor_lower, True), projected)
        image_field = product - deflation_image(correction)
        return (image_field, norm_value, cross_value - jnp.sum(projected * correction))

    image_field, norm_now, curvature_now = joint_terms(residual)
    step_size = norm_now / curvature_now
    direction = residual
    along = image_field
    for iteration in range(ITERS):
        estimate = estimate + step_size * direction
        residual = residual - step_size * along
        if iteration + 1 < ITERS:
            image_field, norm_next, curvature_now = joint_terms(residual)
            step_ratio = norm_next / norm_now
            step_size = norm_next / (curvature_now - step_ratio * norm_next / step_size)
            direction = residual + step_ratio * direction
            along = image_field + step_ratio * along
            norm_now = norm_next
    solution = coarse_part + estimate - prolong(coarse_solve(apply_field(estimate)))
    return (solution, residual)


def solution(mesh):
    placed = (P("gx", "gy", "gz"), P("gx", "gy", "gz"), P("gx", "gy", "gz"), P(), P())
    return jax.shard_map(
        body,
        mesh=mesh,
        in_specs=placed,
        out_specs=(P("gx", "gy", "gz"), P("gx", "gy", "gz")),
        check_vma=False,
    )
```

profile of v0, /device:TPU:0, one launch (start us, length us, event | category | flops | bytes accessed | tf_op | source)
XLA Modules:
  0.0 365.0 jit_solution(11324183408643841926)
XLA Ops:
  1.6 1.7 select_reduce_fusion
  4.2 4.9 %collective-permute-start = (f32[6,1,16,128]{3,2,1,0:T(8,128)S(1)}, f32[6,1,16,128]{3,2,1,0:T(8,128)S(1)}, u32[]{:S(2)}, u32[]{:S(2)}) collective-permute-start(f32[6,1,16,128]{3,2,1,0:T(8,128)S(1)} %get-tuple-element.39), channel_id=1, source_target_pairs={{0,16},{1,17},{2,18},{3,19},{4,20},{5,21},{6,22},{7,23},{8,24},{9,... | collective-permute-start | bytes 147464 | tf_op jit(solution)/shard_map/ppermute | solution.py:44
  11.4 3.7 %collective-permute-done.1 = f32[6,1,16,128]{3,2,1,0:T(8,128)S(1)} collective-permute-done((f32[6,1,16,128]{3,2,1,0:T(8,128)S(1)}, f32[6,1,16,128]{3,2,1,0:T(8,128)S(1)}, u32[]{:S(2)}, u32[]{:S(2)}) %collective-permute-start.1) | collective-permute-done | bytes 49184 | tf_op jit(solution)/shard_map/ppermute | solution.py:46
  15.1 3.5 collective-permute-start.2
  20.2 4.2 %collective-permute-done.3 = f32[6,10,1,128]{3,2,1,0:T(1,128)S(1)} collective-permute-done((f32[6,10,1,128]{3,2,1,0:T(1,128)S(1)}, f32[6,10,1,128]{3,2,1,0:T(1,128)S(1)}, u32[]{:S(2)}, u32[]{:S(2)}) %collective-permute-start.3) | collective-permute-done | bytes 30752 | tf_op jit(solution)/shard_map/ppermute | solution.py:46
  28.8 3.0 collective-permute-done.5
  43.4 40.4 %all-reduce.3 = (f32[64,64]{1,0:T(8,128)S(1)}, f32[64]{0:T(128)S(1)}) all-reduce(f32[64,64]{1,0:T(8,128)S(1)} %convolution_subtract_fusion, f32[64]{0:T(128)S(1)} %convolution_bitcast_fusion.26), channel_id=1, replica_groups=mesh['gx'=2,'gy'=4,'gz'=4] {'gx','gy','gz'}, use_global_device_ids=true, to_apply=%region_7.8 | all-reduce | flops 4160 | bytes 33280 | tf_op jit(solution)/shard_map/psum | solution.py:154
  84.0 5.8 %cholesky.19 = f32[64,64]{1,0:T(8,128)S(1)} custom-call(f32[64,64]{1,0:T(8,128)S(1)} %fusion.262), custom_call_target="Cholesky" | custom-call | tf_op jit(solution)/shard_map/jit(cholesky)/cholesky | solution.py:156
  91.2 4.9 %custom-call.11 = f32[1,64,64]{1,2,0:T(8,128)S(1)} custom-call(f32[1,64,64]{2,1,0:T(8,128)S(1)} %fusion.251), custom_call_target="InvertDiagBlocksLowerTriangular" | custom-call | tf_op jit(solution)/shard_map/jit(_cho_solve)/triangular_solve | solution.py:172
  98.1 4.5 %collective-permute-start.7 = (f32[1,16,128]{2,1,0:T(8,128)S(1)}, f32[1,16,128]{2,1,0:T(8,128)S(1)}, u32[]{:S(2)}, u32[]{:S(2)}) collective-permute-start(f32[1,16,128]{2,1,0:T(8,128)S(1)} %slice.1082), channel_id=1, source_target_pairs={{0,16},{1,17},{2,18},{3,19},{4,20},{5,21},{6,22},{7,23},{8,24},{9,... | collective-permute-start | bytes 24584 | tf_op jit(solution)/shard_map/ppermute | solution.py:44
  102.6 1.3 collective-permute-done.7
  105.3 4.5 %collective-permute-start.9 = (f32[10,1,128]{2,1,0:T(1,128)S(1)}, f32[10,1,128]{2,1,0:T(1,128)S(1)}, u32[]{:S(2)}, u32[]{:S(2)}) collective-permute-start(f32[10,1,128]{2,1,0:T(1,128)S(1)} %get-tuple-element.105), channel_id=1, source_target_pairs={{0,4},{4,8},{8,12},{1,5},{5,9},{9,13},{2,6},{6,10},{10,14},{3,7},{... | collective-permute-start | bytes 15368 | tf_op jit(solution)/shard_map/ppermute | solution.py:44
  112.6 3.0 collective-permute-start.11
  118.3 4.5 %collective-permute-start.13 = (f32[1,16,128]{2,1,0:T(8,128)S(1)}, f32[1,16,128]{2,1,0:T(8,128)S(1)}, u32[]{:S(2)}, u32[]{:S(2)}) collective-permute-start(f32[1,16,128]{2,1,0:T(8,128)S(1)} %get-tuple-element.111), channel_id=1, source_target_pairs={{0,16},{1,17},{2,18},{3,19},{4,20},{5,21},{6,22},{7,23},{8,24},{9,... | collective-permute-start | bytes 24584 | tf_op jit(solution)/shard_map/ppermute | solution.py:44
  122.9 1.3 collective-permute-done.13
  125.5 4.8 %collective-permute-start.15 = (f32[10,1,128]{2,1,0:T(1,128)S(1)}, f32[10,1,128]{2,1,0:T(1,128)S(1)}, u32[]{:S(2)}, u32[]{:S(2)}) collective-permute-start(f32[10,1,128]{2,1,0:T(1,128)S(1)} %get-tuple-element.101), channel_id=1, source_target_pairs={{0,4},{4,8},{8,12},{1,5},{5,9},{9,13},{2,6},{6,10},{10,14},{3,7},{... | collective-permute-start | bytes 15368 | tf_op jit(solution)/shard_map/ppermute | solution.py:44
  133.1 3.3 collective-permute-start.17
  138.8 48.9 %all-reduce.2 = (f32[64]{0:T(128)S(1)}, f32[]{:T(128)}, f32[]{:T(128)}) all-reduce(f32[64]{0:T(128)S(1)} %convolution_bitcast_fusion.24, f32[]{:T(128)} %get-tuple-element.10, f32[]{:T(128)} %get-tuple-element.8), channel_id=1, replica_groups=mesh['gx'=2,'gy'=4,'gz'=4] {'gx','gy','gz'}, use_global_device_ids=true, to_apply=%region_19.21 | all-reduce | flops 66 | bytes 528 | tf_op jit(solution)/shard_map/psum | solution.py:185
  190.3 4.5 %collective-permute-start.19 = (f32[1,16,128]{2,1,0:T(8,128)S(1)}, f32[1,16,128]{2,1,0:T(8,128)S(1)}, u32[]{:S(2)}, u32[]{:S(2)}) collective-permute-start(f32[1,16,128]{2,1,0:T(8,128)S(1)} %slice.1129), channel_id=1, source_target_pairs={{0,16},{1,17},{2,18},{3,19},{4,20},{5,21},{6,22},{7,23},{8,24},{9,... | collective-permute-start | bytes 24584 | tf_op jit(solution)/shard_map/ppermute | solution.py:44
  197.5 4.5 %collective-permute-start.21 = (f32[10,1,128]{2,1,0:T(1,128)S(1)}, f32[10,1,128]{2,1,0:T(1,128)S(1)}, u32[]{:S(2)}, u32[]{:S(2)}) collective-permute-start(f32[10,1,128]{2,1,0:T(1,128)S(1)} %get-tuple-element.97), channel_id=1, source_target_pairs={{0,4},{4,8},{8,12},{1,5},{5,9},{9,13},{2,6},{6,10},{10,14},{3,7},{... | collective-permute-start | bytes 15368 | tf_op jit(solution)/shard_map/ppermute | solution.py:44
  205.5 3.0 collective-permute-start.23
  211.2 4.5 %collective-permute-start.25 = (f32[1,16,128]{2,1,0:T(8,128)S(1)}, f32[1,16,128]{2,1,0:T(8,128)S(1)}, u32[]{:S(2)}, u32[]{:S(2)}) collective-permute-start(f32[1,16,128]{2,1,0:T(8,128)S(1)} %get-tuple-element.109), channel_id=1, source_target_pairs={{0,16},{1,17},{2,18},{3,19},{4,20},{5,21},{6,22},{7,23},{8,24},{9,... | collective-permute-start | bytes 24584 | tf_op jit(solution)/shard_map/ppermute | solution.py:44
  218.4 4.5 %collective-permute-start.27 = (f32[10,1,128]{2,1,0:T(1,128)S(1)}, f32[10,1,128]{2,1,0:T(1,128)S(1)}, u32[]{:S(2)}, u32[]{:S(2)}) collective-permute-start(f32[10,1,128]{2,1,0:T(1,128)S(1)} %get-tuple-element.93), channel_id=1, source_target_pairs={{0,4},{4,8},{8,12},{1,5},{5,9},{9,13},{2,6},{6,10},{10,14},{3,7},{... | collective-permute-start | bytes 15368 | tf_op jit(solution)/shard_map/ppermute | solution.py:44
  225.7 3.2 collective-permute-start.29
  231.3 48.6 %all-reduce.1 = (f32[]{:T(128)}, f32[]{:T(128)}, f32[64]{0:T(128)S(1)}) all-reduce(f32[]{:T(128)} %get-tuple-element.7, f32[]{:T(128)} %get-tuple-element.6, f32[64]{0:T(128)S(1)} %convolution_bitcast_fusion.22), channel_id=1, replica_groups=mesh['gx'=2,'gy'=4,'gz'=4] {'gx','gy','gz'}, use_global_device_ids=true, to_apply=%region_22.24 | all-reduce | flops 66 | bytes 528 | tf_op jit(solution)/shard_map/psum | solution.py:185
  282.6 4.5 %collective-permute-start.37 = (f32[1,16,128]{2,1,0:T(8,128)S(1)}, f32[1,16,128]{2,1,0:T(8,128)S(1)}, u32[]{:S(2)}, u32[]{:S(2)}) collective-permute-start(f32[1,16,128]{2,1,0:T(8,128)S(1)} %slice.1200), channel_id=1, source_target_pairs={{0,16},{1,17},{2,18},{3,19},{4,20},{5,21},{6,22},{7,23},{8,24},{9,... | collective-permute-start | bytes 24584 | tf_op jit(solution)/shard_map/ppermute | solution.py:44
  293.0 4.5 %collective-permute-start.31 = (f32[1,16,128]{2,1,0:T(8,128)S(1)}, f32[1,16,128]{2,1,0:T(8,128)S(1)}, u32[]{:S(2)}, u32[]{:S(2)}) collective-permute-start(f32[1,16,128]{2,1,0:T(8,128)S(1)} %get-tuple-element.107), channel_id=1, source_target_pairs={{0,16},{1,17},{2,18},{3,19},{4,20},{5,21},{6,22},{7,23},{8,24},{9,... | collective-permute-start | bytes 24584 | tf_op jit(solution)/shard_map/ppermute | solution.py:44
  298.9 4.5 %collective-permute-start.39 = (f32[10,1,128]{2,1,0:T(1,128)S(1)}, f32[10,1,128]{2,1,0:T(1,128)S(1)}, u32[]{:S(2)}, u32[]{:S(2)}) collective-permute-start(f32[10,1,128]{2,1,0:T(1,128)S(1)} %get-tuple-element.85), channel_id=1, source_target_pairs={{0,4},{4,8},{8,12},{1,5},{5,9},{9,13},{2,6},{6,10},{10,14},{3,7},{... | collective-permute-start | bytes 15368 | tf_op jit(solution)/shard_map/ppermute | solution.py:44
  304.8 4.5 %collective-permute-start.33 = (f32[10,1,128]{2,1,0:T(1,128)S(1)}, f32[10,1,128]{2,1,0:T(1,128)S(1)}, u32[]{:S(2)}, u32[]{:S(2)}) collective-permute-start(f32[10,1,128]{2,1,0:T(1,128)S(1)} %get-tuple-element.89), channel_id=1, source_target_pairs={{0,4},{4,8},{8,12},{1,5},{5,9},{9,13},{2,6},{6,10},{10,14},{3,7},{... | collective-permute-start | bytes 15368 | tf_op jit(solution)/shard_map/ppermute | solution.py:44
  310.8 3.0 collective-permute-start.41
  315.3 4.7 %collective-permute-start.35 = (f32[10,18,1]{2,1,0:T(8,128)S(1)}, f32[10,18,1]{2,1,0:T(8,128)S(1)}, u32[]{:S(2)}, u32[]{:S(2)}) collective-permute-start(f32[10,18,1]{2,1,0:T(8,128)S(1)} %get-tuple-element.61), channel_id=1, source_target_pairs={{0,1},{1,2},{2,3},{4,5},{5,6},{6,7},{8,9},{9,10},{10,11},{12,13},{... | collective-permute-start | bytes 2168 | tf_op jit(solution)/shard_map/ppermute | solution.py:44
  321.7 40.9 %psum.71 = f32[64]{0:T(128)S(1)} all-reduce(f32[64]{0:T(128)S(1)} %convolution_bitcast_fusion.21), channel_id=1, replica_groups=mesh['gx'=2,'gy'=4,'gz'=4] {'gx','gy','gz'}, use_global_device_ids=true, to_apply=%region_31.33 | all-reduce | flops 64 | bytes 512 | tf_op jit(solution)/shard_map/psum | solution.py:171
  (248 shorter events, 68.3 us)
Async XLA Ops:
  4.2 7.1 %collective-permute-start = (f32[6,1,16,128]{3,2,1,0:T(8,128)S(1)}, f32[6,1,16,128]{3,2,1,0:T(8,128)S(1)}, u32[]{:S(2)}, u32[]{:S(2)}) collective-permute-start(f32[6,1,16,128]{3,2,1,0:T(8,128)S(1)} %get-tuple-element.39), channel_id=1, source_target_pairs={{0,16},{1,17},{2,18},{3,19},{4,20},{5,21},{6,22},{7,23},{8,24},{9,... | collective-permute-start | bytes 147464 | tf_op jit(solution)/shard_map/ppermute | solution.py:44
  9.1 6.0 %collective-permute-start.1 = (f32[6,1,16,128]{3,2,1,0:T(8,128)S(1)}, f32[6,1,16,128]{3,2,1,0:T(8,128)S(1)}, u32[]{:S(2)}, u32[]{:S(2)}) collective-permute-start(f32[6,1,16,128]{3,2,1,0:T(8,128)S(1)} %get-tuple-element.40), channel_id=1, source_target_pairs={{16,0},{17,1},{18,2},{19,3},{20,4},{21,5},{22,6},{23,7},{24,8},{25... | collective-permute-start | bytes 147464 | tf_op jit(solution)/shard_map/ppermute | solution.py:46
  15.1 5.0 %collective-permute-start.2 = (f32[6,10,1,128]{3,2,1,0:T(1,128)S(1)}, f32[6,10,1,128]{3,2,1,0:T(1,128)S(1)}, u32[]{:S(2)}, u32[]{:S(2)}) collective-permute-start(f32[6,10,1,128]{3,2,1,0:T(1,128)S(1)} %get-tuple-element.37), channel_id=1, source_target_pairs={{0,4},{4,8},{8,12},{1,5},{5,9},{9,13},{2,6},{6,10},{10,14},{3,7},{... | collective-permute-start | bytes 92168 | tf_op jit(solution)/shard_map/ppermute | solution.py:44
  18.6 5.8 %collective-permute-start.3 = (f32[6,10,1,128]{3,2,1,0:T(1,128)S(1)}, f32[6,10,1,128]{3,2,1,0:T(1,128)S(1)}, u32[]{:S(2)}, u32[]{:S(2)}) collective-permute-start(f32[6,10,1,128]{3,2,1,0:T(1,128)S(1)} %get-tuple-element.38), channel_id=1, source_target_pairs={{4,0},{8,4},{12,8},{5,1},{9,5},{13,9},{6,2},{10,6},{14,10},{7,3},{... | collective-permute-start | bytes 92168 | tf_op jit(solution)/shard_map/ppermute | solution.py:46
  96.8 5.9 %collective-permute-start.6 = (f32[1,16,128]{2,1,0:T(8,128)S(1)}, f32[1,16,128]{2,1,0:T(8,128)S(1)}, u32[]{:S(2)}, u32[]{:S(2)}) collective-permute-start(f32[1,16,128]{2,1,0:T(8,128)S(1)} %slice.1082), channel_id=1, source_target_pairs={{16,0},{17,1},{18,2},{19,3},{20,4},{21,5},{22,6},{23,7},{24,8},{25... | collective-permute-start | bytes 24584 | tf_op jit(solution)/shard_map/ppermute | solution.py:46
  98.1 5.9 %collective-permute-start.7 = (f32[1,16,128]{2,1,0:T(8,128)S(1)}, f32[1,16,128]{2,1,0:T(8,128)S(1)}, u32[]{:S(2)}, u32[]{:S(2)}) collective-permute-start(f32[1,16,128]{2,1,0:T(8,128)S(1)} %slice.1082), channel_id=1, source_target_pairs={{0,16},{1,17},{2,18},{3,19},{4,20},{5,21},{6,22},{7,23},{8,24},{9,... | collective-permute-start | bytes 24584 | tf_op jit(solution)/shard_map/ppermute | solution.py:44
  104.0 5.9 %collective-permute-start.8 = (f32[10,1,128]{2,1,0:T(1,128)S(1)}, f32[10,1,128]{2,1,0:T(1,128)S(1)}, u32[]{:S(2)}, u32[]{:S(2)}) collective-permute-start(f32[10,1,128]{2,1,0:T(1,128)S(1)} %get-tuple-element.106), channel_id=1, source_target_pairs={{4,0},{8,4},{12,8},{5,1},{9,5},{13,9},{6,2},{10,6},{14,10},{7,3},{... | collective-permute-start | bytes 15368 | tf_op jit(solution)/shard_map/ppermute | solution.py:46
  105.3 5.9 %collective-permute-start.9 = (f32[10,1,128]{2,1,0:T(1,128)S(1)}, f32[10,1,128]{2,1,0:T(1,128)S(1)}, u32[]{:S(2)}, u32[]{:S(2)}) collective-permute-start(f32[10,1,128]{2,1,0:T(1,128)S(1)} %get-tuple-element.105), channel_id=1, source_target_pairs={{0,4},{4,8},{8,12},{1,5},{5,9},{9,13},{2,6},{6,10},{10,14},{3,7},{... | collective-permute-start | bytes 15368 | tf_op jit(solution)/shard_map/ppermute | solution.py:44
  117.0 5.9 %collective-permute-start.12 = (f32[1,16,128]{2,1,0:T(8,128)S(1)}, f32[1,16,128]{2,1,0:T(8,128)S(1)}, u32[]{:S(2)}, u32[]{:S(2)}) collective-permute-start(f32[1,16,128]{2,1,0:T(8,128)S(1)} %get-tuple-element.112), channel_id=1, source_target_pairs={{16,0},{17,1},{18,2},{19,3},{20,4},{21,5},{22,6},{23,7},{24,8},{25... | collective-permute-start | bytes 24584 | tf_op jit(solution)/shard_map/ppermute | solution.py:46
  118.3 5.9 %collective-permute-start.13 = (f32[1,16,128]{2,1,0:T(8,128)S(1)}, f32[1,16,128]{2,1,0:T(8,128)S(1)}, u32[]{:S(2)}, u32[]{:S(2)}) collective-permute-start(f32[1,16,128]{2,1,0:T(8,128)S(1)} %get-tuple-element.111), channel_id=1, source_target_pairs={{0,16},{1,17},{2,18},{3,19},{4,20},{5,21},{6,22},{7,23},{8,24},{9,... | collective-permute-start | bytes 24584 | tf_op jit(solution)/shard_map/ppermute | solution.py:44
  124.2 6.1 %collective-permute-start.14 = (f32[10,1,128]{2,1,0:T(1,128)S(1)}, f32[10,1,128]{2,1,0:T(1,128)S(1)}, u32[]{:S(2)}, u32[]{:S(2)}) collective-permute-start(f32[10,1,128]{2,1,0:T(1,128)S(1)} %get-tuple-element.102), channel_id=1, source_target_pairs={{4,0},{8,4},{12,8},{5,1},{9,5},{13,9},{6,2},{10,6},{14,10},{7,3},{... | collective-permute-start | bytes 15368 | tf_op jit(solution)/shard_map/ppermute | solution.py:46
  125.5 6.1 %collective-permute-start.15 = (f32[10,1,128]{2,1,0:T(1,128)S(1)}, f32[10,1,128]{2,1,0:T(1,128)S(1)}, u32[]{:S(2)}, u32[]{:S(2)}) collective-permute-start(f32[10,1,128]{2,1,0:T(1,128)S(1)} %get-tuple-element.101), channel_id=1, source_target_pairs={{0,4},{4,8},{8,12},{1,5},{5,9},{9,13},{2,6},{6,10},{10,14},{3,7},{... | collective-permute-start | bytes 15368 | tf_op jit(solution)/shard_map/ppermute | solution.py:44
  189.0 5.8 %collective-permute-start.18 = (f32[1,16,128]{2,1,0:T(8,128)S(1)}, f32[1,16,128]{2,1,0:T(8,128)S(1)}, u32[]{:S(2)}, u32[]{:S(2)}) collective-permute-start(f32[1,16,128]{2,1,0:T(8,128)S(1)} %slice.1129), channel_id=1, source_target_pairs={{16,0},{17,1},{18,2},{19,3},{20,4},{21,5},{22,6},{23,7},{24,8},{25... | collective-permute-start | bytes 24584 | tf_op jit(solution)/shard_map/ppermute | solution.py:46
  190.3 5.9 %collective-permute-start.19 = (f32[1,16,128]{2,1,0:T(8,128)S(1)}, f32[1,16,128]{2,1,0:T(8,128)S(1)}, u32[]{:S(2)}, u32[]{:S(2)}) collective-permute-start(f32[1,16,128]{2,1,0:T(8,128)S(1)} %slice.1129), channel_id=1, source_target_pairs={{0,16},{1,17},{2,18},{3,19},{4,20},{5,21},{6,22},{7,23},{8,24},{9,... | collective-permute-start | bytes 24584 | tf_op jit(solution)/shard_map/ppermute | solution.py:44
  196.2 7.8 %collective-permute-start.20 = (f32[10,1,128]{2,1,0:T(1,128)S(1)}, f32[10,1,128]{2,1,0:T(1,128)S(1)}, u32[]{:S(2)}, u32[]{:S(2)}) collective-permute-start(f32[10,1,128]{2,1,0:T(1,128)S(1)} %get-tuple-element.98), channel_id=1, source_target_pairs={{4,0},{8,4},{12,8},{5,1},{9,5},{13,9},{6,2},{10,6},{14,10},{7,3},{... | collective-permute-start | bytes 15368 | tf_op jit(solution)/shard_map/ppermute | solution.py:46
  197.5 6.5 %collective-permute-start.21 = (f32[10,1,128]{2,1,0:T(1,128)S(1)}, f32[10,1,128]{2,1,0:T(1,128)S(1)}, u32[]{:S(2)}, u32[]{:S(2)}) collective-permute-start(f32[10,1,128]{2,1,0:T(1,128)S(1)} %get-tuple-element.97), channel_id=1, source_target_pairs={{0,4},{4,8},{8,12},{1,5},{5,9},{9,13},{2,6},{6,10},{10,14},{3,7},{... | collective-permute-start | bytes 15368 | tf_op jit(solution)/shard_map/ppermute | solution.py:44
  209.9 5.9 %collective-permute-start.24 = (f32[1,16,128]{2,1,0:T(8,128)S(1)}, f32[1,16,128]{2,1,0:T(8,128)S(1)}, u32[]{:S(2)}, u32[]{:S(2)}) collective-permute-start(f32[1,16,128]{2,1,0:T(8,128)S(1)} %get-tuple-element.110), channel_id=1, source_target_pairs={{16,0},{17,1},{18,2},{19,3},{20,4},{21,5},{22,6},{23,7},{24,8},{25... | collective-permute-start | bytes 24584 | tf_op jit(solution)/shard_map/ppermute | solution.py:46
  211.2 5.9 %collective-permute-start.25 = (f32[1,16,128]{2,1,0:T(8,128)S(1)}, f32[1,16,128]{2,1,0:T(8,128)S(1)}, u32[]{:S(2)}, u32[]{:S(2)}) collective-permute-start(f32[1,16,128]{2,1,0:T(8,128)S(1)} %get-tuple-element.109), channel_id=1, source_target_pairs={{0,16},{1,17},{2,18},{3,19},{4,20},{5,21},{6,22},{7,23},{8,24},{9,... | collective-permute-start | bytes 24584 | tf_op jit(solution)/shard_map/ppermute | solution.py:44
  217.1 5.9 %collective-permute-start.26 = (f32[10,1,128]{2,1,0:T(1,128)S(1)}, f32[10,1,128]{2,1,0:T(1,128)S(1)}, u32[]{:S(2)}, u32[]{:S(2)}) collective-permute-start(f32[10,1,128]{2,1,0:T(1,128)S(1)} %get-tuple-element.94), channel_id=1, source_target_pairs={{4,0},{8,4},{12,8},{5,1},{9,5},{13,9},{6,2},{10,6},{14,10},{7,3},{... | collective-permute-start | bytes 15368 | tf_op jit(solution)/shard_map/ppermute | solution.py:46
  218.4 5.9 %collective-permute-start.27 = (f32[10,1,128]{2,1,0:T(1,128)S(1)}, f32[10,1,128]{2,1,0:T(1,128)S(1)}, u32[]{:S(2)}, u32[]{:S(2)}) collective-permute-start(f32[10,1,128]{2,1,0:T(1,128)S(1)} %get-tuple-element.93), channel_id=1, source_target_pairs={{0,4},{4,8},{8,12},{1,5},{5,9},{9,13},{2,6},{6,10},{10,14},{3,7},{... | collective-permute-start | bytes 15368 | tf_op jit(solution)/shard_map/ppermute | solution.py:44
  281.3 16.3 %collective-permute-start.36 = (f32[1,16,128]{2,1,0:T(8,128)S(1)}, f32[1,16,128]{2,1,0:T(8,128)S(1)}, u32[]{:S(2)}, u32[]{:S(2)}) collective-permute-start(f32[1,16,128]{2,1,0:T(8,128)S(1)} %slice.1200), channel_id=1, source_target_pairs={{16,0},{17,1},{18,2},{19,3},{20,4},{21,5},{22,6},{23,7},{24,8},{25... | collective-permute-start | bytes 24584 | tf_op jit(solution)/shard_map/ppermute | solution.py:46
  282.6 15.0 %collective-permute-start.37 = (f32[1,16,128]{2,1,0:T(8,128)S(1)}, f32[1,16,128]{2,1,0:T(8,128)S(1)}, u32[]{:S(2)}, u32[]{:S(2)}) collective-permute-start(f32[1,16,128]{2,1,0:T(8,128)S(1)} %slice.1200), channel_id=1, source_target_pairs={{0,16},{1,17},{2,18},{3,19},{4,20},{5,21},{6,22},{7,23},{8,24},{9,... | collective-permute-start | bytes 24584 | tf_op jit(solution)/shard_map/ppermute | solution.py:44
  291.7 11.8 %collective-permute-start.30 = (f32[1,16,128]{2,1,0:T(8,128)S(1)}, f32[1,16,128]{2,1,0:T(8,128)S(1)}, u32[]{:S(2)}, u32[]{:S(2)}) collective-permute-start(f32[1,16,128]{2,1,0:T(8,128)S(1)} %get-tuple-element.108), channel_id=1, source_target_pairs={{16,0},{17,1},{18,2},{19,3},{20,4},{21,5},{22,6},{23,7},{24,8},{25... | collective-permute-start | bytes 24584 | tf_op jit(solution)/shard_map/ppermute | solution.py:46
  293.0 10.5 %collective-permute-start.31 = (f32[1,16,128]{2,1,0:T(8,128)S(1)}, f32[1,16,128]{2,1,0:T(8,128)S(1)}, u32[]{:S(2)}, u32[]{:S(2)}) collective-permute-start(f32[1,16,128]{2,1,0:T(8,128)S(1)} %get-tuple-element.107), channel_id=1, source_target_pairs={{0,16},{1,17},{2,18},{3,19},{4,20},{5,21},{6,22},{7,23},{8,24},{9,... | collective-permute-start | bytes 24584 | tf_op jit(solution)/shard_map/ppermute | solution.py:44
  297.6 11.8 %collective-permute-start.38 = (f32[10,1,128]{2,1,0:T(1,128)S(1)}, f32[10,1,128]{2,1,0:T(1,128)S(1)}, u32[]{:S(2)}, u32[]{:S(2)}) collective-permute-start(f32[10,1,128]{2,1,0:T(1,128)S(1)} %get-tuple-element.86), channel_id=1, source_target_pairs={{4,0},{8,4},{12,8},{5,1},{9,5},{13,9},{6,2},{10,6},{14,10},{7,3},{... | collective-permute-start | bytes 15368 | tf_op jit(solution)/shard_map/ppermute | solution.py:46
  298.9 10.5 %collective-permute-start.39 = (f32[10,1,128]{2,1,0:T(1,128)S(1)}, f32[10,1,128]{2,1,0:T(1,128)S(1)}, u32[]{:S(2)}, u32[]{:S(2)}) collective-permute-start(f32[10,1,128]{2,1,0:T(1,128)S(1)} %get-tuple-element.85), channel_id=1, source_target_pairs={{0,4},{4,8},{8,12},{1,5},{5,9},{9,13},{2,6},{6,10},{10,14},{3,7},{... | collective-permute-start | bytes 15368 | tf_op jit(solution)/shard_map/ppermute | solution.py:44
  303.5 10.3 %collective-permute-start.32 = (f32[10,1,128]{2,1,0:T(1,128)S(1)}, f32[10,1,128]{2,1,0:T(1,128)S(1)}, u32[]{:S(2)}, u32[]{:S(2)}) collective-permute-start(f32[10,1,128]{2,1,0:T(1,128)S(1)} %get-tuple-element.90), channel_id=1, source_target_pairs={{4,0},{8,4},{12,8},{5,1},{9,5},{13,9},{6,2},{10,6},{14,10},{7,3},{... | collective-permute-start | bytes 15368 | tf_op jit(solution)/shard_map/ppermute | solution.py:46
  304.8 9.1 %collective-permute-start.33 = (f32[10,1,128]{2,1,0:T(1,128)S(1)}, f32[10,1,128]{2,1,0:T(1,128)S(1)}, u32[]{:S(2)}, u32[]{:S(2)}) collective-permute-start(f32[10,1,128]{2,1,0:T(1,128)S(1)} %get-tuple-element.89), channel_id=1, source_target_pairs={{0,4},{4,8},{8,12},{1,5},{5,9},{9,13},{2,6},{6,10},{10,14},{3,7},{... | collective-permute-start | bytes 15368 | tf_op jit(solution)/shard_map/ppermute | solution.py:44
  309.5 54.4 %collective-permute-start.40 = (f32[10,18,1]{2,1,0:T(8,128)S(1)}, f32[10,18,1]{2,1,0:T(8,128)S(1)}, u32[]{:S(2)}, u32[]{:S(2)}) collective-permute-start(f32[10,18,1]{2,1,0:T(8,128)S(1)} %get-tuple-element.60), channel_id=1, source_target_pairs={{1,0},{2,1},{3,2},{5,4},{6,5},{7,6},{9,8},{10,9},{11,10},{13,12},{... | collective-permute-start | bytes 2168 | tf_op jit(solution)/shard_map/ppermute | solution.py:46
  310.8 53.1 %collective-permute-start.41 = (f32[10,18,1]{2,1,0:T(8,128)S(1)}, f32[10,18,1]{2,1,0:T(8,128)S(1)}, u32[]{:S(2)}, u32[]{:S(2)}) collective-permute-start(f32[10,18,1]{2,1,0:T(8,128)S(1)} %get-tuple-element.59), channel_id=1, source_target_pairs={{0,1},{1,2},{2,3},{4,5},{5,6},{6,7},{8,9},{9,10},{10,11},{12,13},{... | collective-permute-start | bytes 2168 | tf_op jit(solution)/shard_map/ppermute | solution.py:44
  314.0 6.0 %collective-permute-start.34 = (f32[10,18,1]{2,1,0:T(8,128)S(1)}, f32[10,18,1]{2,1,0:T(8,128)S(1)}, u32[]{:S(2)}, u32[]{:S(2)}) collective-permute-start(f32[10,18,1]{2,1,0:T(8,128)S(1)} %get-tuple-element.62), channel_id=1, source_target_pairs={{1,0},{2,1},{3,2},{5,4},{6,5},{7,6},{9,8},{10,9},{11,10},{13,12},{... | collective-permute-start | bytes 2168 | tf_op jit(solution)/shard_map/ppermute | solution.py:46
  315.3 5.6 %collective-permute-start.35 = (f32[10,18,1]{2,1,0:T(8,128)S(1)}, f32[10,18,1]{2,1,0:T(8,128)S(1)}, u32[]{:S(2)}, u32[]{:S(2)}) collective-permute-start(f32[10,18,1]{2,1,0:T(8,128)S(1)} %get-tuple-element.61), channel_id=1, source_target_pairs={{0,1},{1,2},{2,3},{4,5},{5,6},{6,7},{8,9},{9,10},{10,11},{12,13},{... | collective-permute-start | bytes 2168 | tf_op jit(solution)/shard_map/ppermute | solution.py:44
  (12 other events, 62.7 us)
where the time goes:
time: 367 us; the launch traced here: 365 us
  blocking collectives  179 us (49%)
  starting transfers between devices  112 us (31%)
  waiting for transfers between devices  25.1 us (7%)
  other arithmetic  22.3 us (6%)
  matrix products  13.4 us (4%)
  between operations  8.31 us (2%)
  local copies, waits for them, and re-layouts  5.09 us (1%)
    psum x2, blocking collectives, joint_terms(): lax.psum((restrict(product), jnp.sum(field * field), jnp.sum(field * prod...  97.5 us
    ppermute x21, starting transfers between devices, padded_2(): lax.ppermute(tail, axis, [(i, (i + 1) % count) for i in range(ends)])  84.8 us
    psum x1, blocking collectives, coarse_solve(): projected = lax.psum(restrict(field), ('gx', 'gy', 'gz'))  40.9 us
    psum x1, blocking collectives, body(): coarse = lax.psum(jnp.diag(diagonal_terms) - coupling, ('gx', 'gy', 'gz'))  40.4 us
    ppermute x21, starting transfers between devices, padded_2(): lax.ppermute(head, axis, [((i + 1) % count, i) for i in range(ends)])  27.1 us
    ppermute x21, waiting for transfers between devices, padded_2(): lax.ppermute(tail, axis, [(i, (i + 1) % count) for i in range(ends)])  14.1 us
    ppermute x21, waiting for transfers between devices, padded_2(): lax.ppermute(head, axis, [((i + 1) % count, i) for i in range(ends)])  11 us
    dot_general x54, matrix products, body(): jnp.einsum('xyz,xa,yb,zjc->jabc', weight, reach_onehot(CX, step_x), reach...  8.59 us
  transfers between devices with their start and end apart: 42, of which 16 were waited for; matrix products, arithmetic and copies ran while one was open for 1% of the time, Pallas kernels for 0%

commit v1 on v0

--- a/solution.py
+++ b/solution.py
@@ -151,7 +151,9 @@
         class_onehot(neighbours, COARSE),
         precision=highest,
     )
-    coarse = lax.psum(jnp.diag(diagonal_terms) - coupling, ("gx", "gy", "gz"))
+    coarse = jnp.sum(
+        lax.all_gather(jnp.diag(diagonal_terms) - coupling, ("gx", "gy", "gz")), axis=0
+    )
     coarse = 0.5 * (coarse + coarse.T)
     factor_lower = jnp.linalg.cholesky(coarse)
 

time: 367 us -> 408 us (1.11)
  blocking collectives: 179 us -> 223 us
    all_gather x0 -> x1, blocking collectives: none -> 44.6 us  [body(): lax.all_gather(jnp.diag(diagonal_terms) - coupling, ('gx', 'gy', 'gz'))]
    psum x1 -> x2, blocking collectives: 40.9 us -> 82.7 us  [coarse_solve(): projected = lax.psum(restrict(field), ('gx', 'gy', 'gz'))]
    psum x1 -> x0, blocking collectives: 40.4 us -> none  [body(): coarse = lax.psum(jnp.diag(diagonal_terms) - coupling, ('gx', 'gy', 'gz'))]
  transfers between devices with their start and end apart: 42 -> 42, of which waited for: 16 -> 15; matrix products, arithmetic and copies ran while one was open for 1% -> 1% of each run, Pallas kernels for 0% -> 0%
where the time goes in v1:
time: 408 us; the launch traced here: 406 us
  blocking collectives  223 us (55%)
  starting transfers between devices  112 us (27%)
  other arithmetic  22.5 us (6%)
  waiting for transfers between devices  21.9 us (5%)
  matrix products  13.4 us (3%)
  between operations  8.08 us (2%)
  local copies, waits for them, and re-layouts  5.02 us (1%)
    psum x2, blocking collectives, joint_terms(): lax.psum((restrict(product), jnp.sum(field * field), jnp.sum(field * prod...  95.9 us
    ppermute x21, starting transfers between devices, padded_2(): lax.ppermute(tail, axis, [(i, (i + 1) % count) for i in range(ends)])  84.6 us
    psum x2, blocking collectives, coarse_solve(): projected = lax.psum(restrict(field), ('gx', 'gy', 'gz'))  82.7 us
    all_gather x1, blocking collectives, body(): lax.all_gather(jnp.diag(diagonal_terms) - coupling, ('gx', 'gy', 'gz'))  44.6 us
    ppermute x21, starting transfers between devices, padded_2(): lax.ppermute(head, axis, [((i + 1) % count, i) for i in range(ends)])  27.1 us
    ppermute x21, waiting for transfers between devices, padded_2(): lax.ppermute(tail, axis, [(i, (i + 1) % count) for i in range(ends)])  13.9 us
    dot_general x54, matrix products, body(): jnp.einsum('xyz,xa,yb,zjc->jabc', weight, reach_onehot(CX, step_x), reach...  8.59 us
  transfers between devices with their start and end apart: 42, of which 15 were waited for; matrix products, arithmetic and copies ran while one was open for 1% of the time, Pallas kernels for 0%

profile of v1, /device:TPU:0, one launch (start us, length us, event | category | flops | bytes accessed | tf_op | source)
XLA Modules:
  0.0 405.8 jit_solution(12983472376259670186)
XLA Ops:
  1.6 1.7 select_reduce_fusion
  4.2 4.9 %collective-permute-start = (f32[6,1,16,128]{3,2,1,0:T(8,128)S(1)}, f32[6,1,16,128]{3,2,1,0:T(8,128)S(1)}, u32[]{:S(2)}, u32[]{:S(2)}) collective-permute-start(f32[6,1,16,128]{3,2,1,0:T(8,128)S(1)} %get-tuple-element.37), channel_id=1, source_target_pairs={{0,16},{1,17},{2,18},{3,19},{4,20},{5,21},{6,22},{7,23},{8,24},{9,... | collective-permute-start | bytes 147464 | tf_op jit(solution)/shard_map/ppermute | solution.py:44
  11.4 3.7 collective-permute-done.1
  15.1 3.5 collective-permute-start.2
  20.2 4.2 %collective-permute-done.3 = f32[6,10,1,128]{3,2,1,0:T(1,128)S(1)} collective-permute-done((f32[6,10,1,128]{3,2,1,0:T(1,128)S(1)}, f32[6,10,1,128]{3,2,1,0:T(1,128)S(1)}, u32[]{:S(2)}, u32[]{:S(2)}) %collective-permute-start.3) | collective-permute-done | bytes 30752 | tf_op jit(solution)/shard_map/ppermute | solution.py:46
  28.3 42.0 %psum.56 = f32[64]{0:T(128)S(1)} all-reduce(f32[64]{0:T(128)S(1)} %convolution_bitcast_fusion.26), channel_id=1, replica_groups=mesh['gx'=2,'gy'=4,'gz'=4] {'gx','gy','gz'}, use_global_device_ids=true, to_apply=%region_12.13 | all-reduce | flops 64 | bytes 512 | tf_op jit(solution)/shard_map/psum | solution.py:173
  82.4 44.6 %all-gather = f32[2048,64]{1,0:T(8,128)S(1)} all-gather(f32[64,64]{1,0:T(8,128)S(1)} %convolution_subtract_fusion), channel_id=2, replica_groups=mesh['gx'=2,'gy'=4,'gz'=4] {'gx','gy','gz'}, dimensions={0}, use_global_device_ids=true | all-gather | bytes 540672 | tf_op jit(solution)/shard_map/all_gather | solution.py:155
  127.2 5.8 %cholesky.19 = f32[64,64]{1,0:T(8,128)S(1)} custom-call(f32[64,64]{1,0:T(8,128)S(1)} %fusion.263), custom_call_target="Cholesky" | custom-call | tf_op jit(solution)/shard_map/jit(cholesky)/cholesky | solution.py:158
  134.4 4.9 %custom-call.11 = f32[1,64,64]{1,2,0:T(8,128)S(1)} custom-call(f32[1,64,64]{2,1,0:T(8,128)S(1)} %fusion.251), custom_call_target="InvertDiagBlocksLowerTriangular" | custom-call | tf_op jit(solution)/shard_map/jit(_cho_solve)/triangular_solve | solution.py:174
  141.3 4.5 %collective-permute-start.7 = (f32[1,16,128]{2,1,0:T(8,128)S(1)}, f32[1,16,128]{2,1,0:T(8,128)S(1)}, u32[]{:S(2)}, u32[]{:S(2)}) collective-permute-start(f32[1,16,128]{2,1,0:T(8,128)S(1)} %slice.1082), channel_id=1, source_target_pairs={{0,16},{1,17},{2,18},{3,19},{4,20},{5,21},{6,22},{7,23},{8,24},{9,... | collective-permute-start | bytes 24584 | tf_op jit(solution)/shard_map/ppermute | solution.py:44
  145.8 1.3 collective-permute-done.7
  148.5 4.5 %collective-permute-start.9 = (f32[10,1,128]{2,1,0:T(1,128)S(1)}, f32[10,1,128]{2,1,0:T(1,128)S(1)}, u32[]{:S(2)}, u32[]{:S(2)}) collective-permute-start(f32[10,1,128]{2,1,0:T(1,128)S(1)} %get-tuple-element.103), channel_id=1, source_target_pairs={{0,4},{4,8},{8,12},{1,5},{5,9},{9,13},{2,6},{6,10},{10,14},{3,7},{... | collective-permute-start | bytes 15368 | tf_op jit(solution)/shard_map/ppermute | solution.py:44
  155.8 3.0 collective-permute-start.11
  161.5 4.5 %collective-permute-start.13 = (f32[1,16,128]{2,1,0:T(8,128)S(1)}, f32[1,16,128]{2,1,0:T(8,128)S(1)}, u32[]{:S(2)}, u32[]{:S(2)}) collective-permute-start(f32[1,16,128]{2,1,0:T(8,128)S(1)} %get-tuple-element.109), channel_id=1, source_target_pairs={{0,16},{1,17},{2,18},{3,19},{4,20},{5,21},{6,22},{7,23},{8,24},{9,... | collective-permute-start | bytes 24584 | tf_op jit(solution)/shard_map/ppermute | solution.py:44
  166.0 1.3 collective-permute-done.13
  168.7 4.8 %collective-permute-start.15 = (f32[10,1,128]{2,1,0:T(1,128)S(1)}, f32[10,1,128]{2,1,0:T(1,128)S(1)}, u32[]{:S(2)}, u32[]{:S(2)}) collective-permute-start(f32[10,1,128]{2,1,0:T(1,128)S(1)} %get-tuple-element.99), channel_id=1, source_target_pairs={{0,4},{4,8},{8,12},{1,5},{5,9},{9,13},{2,6},{6,10},{10,14},{3,7},{... | collective-permute-start | bytes 15368 | tf_op jit(solution)/shard_map/ppermute | solution.py:44
  176.3 3.2 collective-permute-start.17
  181.7 47.2 %all-reduce.2 = (f32[64]{0:T(128)S(1)}, f32[]{:T(128)}, f32[]{:T(128)}) all-reduce(f32[64]{0:T(128)S(1)} %convolution_bitcast_fusion.24, f32[]{:T(128)} %get-tuple-element.10, f32[]{:T(128)} %get-tuple-element.8), channel_id=1, replica_groups=mesh['gx'=2,'gy'=4,'gz'=4] {'gx','gy','gz'}, use_global_device_ids=true, to_apply=%region_19.21 | all-reduce | flops 66 | bytes 528 | tf_op jit(solution)/shard_map/psum | solution.py:187
  231.4 4.5 %collective-permute-start.19 = (f32[1,16,128]{2,1,0:T(8,128)S(1)}, f32[1,16,128]{2,1,0:T(8,128)S(1)}, u32[]{:S(2)}, u32[]{:S(2)}) collective-permute-start(f32[1,16,128]{2,1,0:T(8,128)S(1)} %slice.1129), channel_id=1, source_target_pairs={{0,16},{1,17},{2,18},{3,19},{4,20},{5,21},{6,22},{7,23},{8,24},{9,... | collective-permute-start | bytes 24584 | tf_op jit(solution)/shard_map/ppermute | solution.py:44
  238.6 4.5 %collective-permute-start.21 = (f32[10,1,128]{2,1,0:T(1,128)S(1)}, f32[10,1,128]{2,1,0:T(1,128)S(1)}, u32[]{:S(2)}, u32[]{:S(2)}) collective-permute-start(f32[10,1,128]{2,1,0:T(1,128)S(1)} %get-tuple-element.95), channel_id=1, source_target_pairs={{0,4},{4,8},{8,12},{1,5},{5,9},{9,13},{2,6},{6,10},{10,14},{3,7},{... | collective-permute-start | bytes 15368 | tf_op jit(solution)/shard_map/ppermute | solution.py:44
  246.5 3.0 collective-permute-start.23
  252.2 4.5 %collective-permute-start.25 = (f32[1,16,128]{2,1,0:T(8,128)S(1)}, f32[1,16,128]{2,1,0:T(8,128)S(1)}, u32[]{:S(2)}, u32[]{:S(2)}) collective-permute-start(f32[1,16,128]{2,1,0:T(8,128)S(1)} %get-tuple-element.107), channel_id=1, source_target_pairs={{0,16},{1,17},{2,18},{3,19},{4,20},{5,21},{6,22},{7,23},{8,24},{9,... | collective-permute-start | bytes 24584 | tf_op jit(solution)/shard_map/ppermute | solution.py:44
  259.4 4.5 %collective-permute-start.27 = (f32[10,1,128]{2,1,0:T(1,128)S(1)}, f32[10,1,128]{2,1,0:T(1,128)S(1)}, u32[]{:S(2)}, u32[]{:S(2)}) collective-permute-start(f32[10,1,128]{2,1,0:T(1,128)S(1)} %get-tuple-element.91), channel_id=1, source_target_pairs={{0,4},{4,8},{8,12},{1,5},{5,9},{9,13},{2,6},{6,10},{10,14},{3,7},{... | collective-permute-start | bytes 15368 | tf_op jit(solution)/shard_map/ppermute | solution.py:44
  266.7 3.2 collective-permute-start.29
  272.4 48.7 %all-reduce.1 = (f32[]{:T(128)}, f32[]{:T(128)}, f32[64]{0:T(128)S(1)}) all-reduce(f32[]{:T(128)} %get-tuple-element.7, f32[]{:T(128)} %get-tuple-element.6, f32[64]{0:T(128)S(1)} %convolution_bitcast_fusion.22), channel_id=1, replica_groups=mesh['gx'=2,'gy'=4,'gz'=4] {'gx','gy','gz'}, use_global_device_ids=true, to_apply=%region_22.24 | all-reduce | flops 66 | bytes 528 | tf_op jit(solution)/shard_map/psum | solution.py:187
  323.8 4.5 %collective-permute-start.37 = (f32[1,16,128]{2,1,0:T(8,128)S(1)}, f32[1,16,128]{2,1,0:T(8,128)S(1)}, u32[]{:S(2)}, u32[]{:S(2)}) collective-permute-start(f32[1,16,128]{2,1,0:T(8,128)S(1)} %slice.1200), channel_id=1, source_target_pairs={{0,16},{1,17},{2,18},{3,19},{4,20},{5,21},{6,22},{7,23},{8,24},{9,... | collective-permute-start | bytes 24584 | tf_op jit(solution)/shard_map/ppermute | solution.py:44
  334.1 4.5 %collective-permute-start.31 = (f32[1,16,128]{2,1,0:T(8,128)S(1)}, f32[1,16,128]{2,1,0:T(8,128)S(1)}, u32[]{:S(2)}, u32[]{:S(2)}) collective-permute-start(f32[1,16,128]{2,1,0:T(8,128)S(1)} %get-tuple-element.105), channel_id=1, source_target_pairs={{0,16},{1,17},{2,18},{3,19},{4,20},{5,21},{6,22},{7,23},{8,24},{9,... | collective-permute-start | bytes 24584 | tf_op jit(solution)/shard_map/ppermute | solution.py:44
  340.0 4.5 %collective-permute-start.39 = (f32[10,1,128]{2,1,0:T(1,128)S(1)}, f32[10,1,128]{2,1,0:T(1,128)S(1)}, u32[]{:S(2)}, u32[]{:S(2)}) collective-permute-start(f32[10,1,128]{2,1,0:T(1,128)S(1)} %get-tuple-element.83), channel_id=1, source_target_pairs={{0,4},{4,8},{8,12},{1,5},{5,9},{9,13},{2,6},{6,10},{10,14},{3,7},{... | collective-permute-start | bytes 15368 | tf_op jit(solution)/shard_map/ppermute | solution.py:44
  345.9 4.5 %collective-permute-start.33 = (f32[10,1,128]{2,1,0:T(1,128)S(1)}, f32[10,1,128]{2,1,0:T(1,128)S(1)}, u32[]{:S(2)}, u32[]{:S(2)}) collective-permute-start(f32[10,1,128]{2,1,0:T(1,128)S(1)} %get-tuple-element.87), channel_id=1, source_target_pairs={{0,4},{4,8},{8,12},{1,5},{5,9},{9,13},{2,6},{6,10},{10,14},{3,7},{... | collective-permute-start | bytes 15368 | tf_op jit(solution)/shard_map/ppermute | solution.py:44
  351.9 3.0 collective-permute-start.41
  356.4 4.6 %collective-permute-start.35 = (f32[10,18,1]{2,1,0:T(8,128)S(1)}, f32[10,18,1]{2,1,0:T(8,128)S(1)}, u32[]{:S(2)}, u32[]{:S(2)}) collective-permute-start(f32[10,18,1]{2,1,0:T(8,128)S(1)} %get-tuple-element.59), channel_id=1, source_target_pairs={{0,1},{1,2},{2,3},{4,5},{5,6},{6,7},{8,9},{9,10},{10,11},{12,13},{... | collective-permute-start | bytes 2168 | tf_op jit(solution)/shard_map/ppermute | solution.py:44
  362.7 40.7 %psum.63 = f32[64]{0:T(128)S(1)} all-reduce(f32[64]{0:T(128)S(1)} %convolution_bitcast_fusion.21), channel_id=1, replica_groups=mesh['gx'=2,'gy'=4,'gz'=4] {'gx','gy','gz'}, use_global_device_ids=true, to_apply=%region_31.33 | all-reduce | flops 64 | bytes 512 | tf_op jit(solution)/shard_map/psum | solution.py:173
  (248 shorter events, 68.2 us)
Async XLA Ops:
  4.2 7.1 %collective-permute-start = (f32[6,1,16,128]{3,2,1,0:T(8,128)S(1)}, f32[6,1,16,128]{3,2,1,0:T(8,128)S(1)}, u32[]{:S(2)}, u32[]{:S(2)}) collective-permute-start(f32[6,1,16,128]{3,2,1,0:T(8,128)S(1)} %get-tuple-element.37), channel_id=1, source_target_pairs={{0,16},{1,17},{2,18},{3,19},{4,20},{5,21},{6,22},{7,23},{8,24},{9,... | collective-permute-start | bytes 147464 | tf_op jit(solution)/shard_map/ppermute | solution.py:44
  9.1 6.0 %collective-permute-start.1 = (f32[6,1,16,128]{3,2,1,0:T(8,128)S(1)}, f32[6,1,16,128]{3,2,1,0:T(8,128)S(1)}, u32[]{:S(2)}, u32[]{:S(2)}) collective-permute-start(f32[6,1,16,128]{3,2,1,0:T(8,128)S(1)} %get-tuple-element.38), channel_id=1, source_target_pairs={{16,0},{17,1},{18,2},{19,3},{20,4},{21,5},{22,6},{23,7},{24,8},{25... | collective-permute-start | bytes 147464 | tf_op jit(solution)/shard_map/ppermute | solution.py:46
  18.6 5.8 %collective-permute-start.3 = (f32[6,10,1,128]{3,2,1,0:T(1,128)S(1)}, f32[6,10,1,128]{3,2,1,0:T(1,128)S(1)}, u32[]{:S(2)}, u32[]{:S(2)}) collective-permute-start(f32[6,10,1,128]{3,2,1,0:T(1,128)S(1)} %get-tuple-element.36), channel_id=1, source_target_pairs={{4,0},{8,4},{12,8},{5,1},{9,5},{13,9},{6,2},{10,6},{14,10},{7,3},{... | collective-permute-start | bytes 92168 | tf_op jit(solution)/shard_map/ppermute | solution.py:46
  25.2 45.1 %collective-permute-start.4 = (f32[6,10,18,1]{2,3,1,0:T(1,128)S(1)}, f32[6,10,18,1]{2,3,1,0:T(1,128)S(1)}, u32[]{:S(2)}, u32[]{:S(2)}) collective-permute-start(f32[6,10,18,1]{2,3,1,0:T(1,128)S(1)} %copy.79), channel_id=1, source_target_pairs={{0,1},{1,2},{2,3},{4,5},{5,6},{6,7},{8,9},{9,10},{10,11},{12,13},{... | collective-permute-start | bytes 12968 | tf_op jit(solution)/shard_map/ppermute | solution.py:44
  27.0 43.8 %collective-permute-start.5 = (f32[6,10,18,1]{2,3,1,0:T(1,128)S(1)}, f32[6,10,18,1]{2,3,1,0:T(1,128)S(1)}, u32[]{:S(2)}, u32[]{:S(2)}) collective-permute-start(f32[6,10,18,1]{2,3,1,0:T(1,128)S(1)} %copy.80), channel_id=1, source_target_pairs={{1,0},{2,1},{3,2},{5,4},{6,5},{7,6},{9,8},{10,9},{11,10},{13,12},{... | collective-permute-start | bytes 12968 | tf_op jit(solution)/shard_map/ppermute | solution.py:46
  140.0 5.9 %collective-permute-start.6 = (f32[1,16,128]{2,1,0:T(8,128)S(1)}, f32[1,16,128]{2,1,0:T(8,128)S(1)}, u32[]{:S(2)}, u32[]{:S(2)}) collective-permute-start(f32[1,16,128]{2,1,0:T(8,128)S(1)} %slice.1082), channel_id=1, source_target_pairs={{16,0},{17,1},{18,2},{19,3},{20,4},{21,5},{22,6},{23,7},{24,8},{25... | collective-permute-start | bytes 24584 | tf_op jit(solution)/shard_map/ppermute | solution.py:46
  141.3 5.9 %collective-permute-start.7 = (f32[1,16,128]{2,1,0:T(8,128)S(1)}, f32[1,16,128]{2,1,0:T(8,128)S(1)}, u32[]{:S(2)}, u32[]{:S(2)}) collective-permute-start(f32[1,16,128]{2,1,0:T(8,128)S(1)} %slice.1082), channel_id=1, source_target_pairs={{0,16},{1,17},{2,18},{3,19},{4,20},{5,21},{6,22},{7,23},{8,24},{9,... | collective-permute-start | bytes 24584 | tf_op jit(solution)/shard_map/ppermute | solution.py:44
  147.2 5.9 %collective-permute-start.8 = (f32[10,1,128]{2,1,0:T(1,128)S(1)}, f32[10,1,128]{2,1,0:T(1,128)S(1)}, u32[]{:S(2)}, u32[]{:S(2)}) collective-permute-start(f32[10,1,128]{2,1,0:T(1,128)S(1)} %get-tuple-element.104), channel_id=1, source_target_pairs={{4,0},{8,4},{12,8},{5,1},{9,5},{13,9},{6,2},{10,6},{14,10},{7,3},{... | collective-permute-start | bytes 15368 | tf_op jit(solution)/shard_map/ppermute | solution.py:46
  148.5 5.9 %collective-permute-start.9 = (f32[10,1,128]{2,1,0:T(1,128)S(1)}, f32[10,1,128]{2,1,0:T(1,128)S(1)}, u32[]{:S(2)}, u32[]{:S(2)}) collective-permute-start(f32[10,1,128]{2,1,0:T(1,128)S(1)} %get-tuple-element.103), channel_id=1, source_target_pairs={{0,4},{4,8},{8,12},{1,5},{5,9},{9,13},{2,6},{6,10},{10,14},{3,7},{... | collective-permute-start | bytes 15368 | tf_op jit(solution)/shard_map/ppermute | solution.py:44
  160.2 5.9 %collective-permute-start.12 = (f32[1,16,128]{2,1,0:T(8,128)S(1)}, f32[1,16,128]{2,1,0:T(8,128)S(1)}, u32[]{:S(2)}, u32[]{:S(2)}) collective-permute-start(f32[1,16,128]{2,1,0:T(8,128)S(1)} %get-tuple-element.110), channel_id=1, source_target_pairs={{16,0},{17,1},{18,2},{19,3},{20,4},{21,5},{22,6},{23,7},{24,8},{25... | collective-permute-start | bytes 24584 | tf_op jit(solution)/shard_map/ppermute | solution.py:46
  161.5 5.9 %collective-permute-start.13 = (f32[1,16,128]{2,1,0:T(8,128)S(1)}, f32[1,16,128]{2,1,0:T(8,128)S(1)}, u32[]{:S(2)}, u32[]{:S(2)}) collective-permute-start(f32[1,16,128]{2,1,0:T(8,128)S(1)} %get-tuple-element.109), channel_id=1, source_target_pairs={{0,16},{1,17},{2,18},{3,19},{4,20},{5,21},{6,22},{7,23},{8,24},{9,... | collective-permute-start | bytes 24584 | tf_op jit(solution)/shard_map/ppermute | solution.py:44
  167.4 6.1 %collective-permute-start.14 = (f32[10,1,128]{2,1,0:T(1,128)S(1)}, f32[10,1,128]{2,1,0:T(1,128)S(1)}, u32[]{:S(2)}, u32[]{:S(2)}) collective-permute-start(f32[10,1,128]{2,1,0:T(1,128)S(1)} %get-tuple-element.100), channel_id=1, source_target_pairs={{4,0},{8,4},{12,8},{5,1},{9,5},{13,9},{6,2},{10,6},{14,10},{7,3},{... | collective-permute-start | bytes 15368 | tf_op jit(solution)/shard_map/ppermute | solution.py:46
  168.7 6.1 %collective-permute-start.15 = (f32[10,1,128]{2,1,0:T(1,128)S(1)}, f32[10,1,128]{2,1,0:T(1,128)S(1)}, u32[]{:S(2)}, u32[]{:S(2)}) collective-permute-start(f32[10,1,128]{2,1,0:T(1,128)S(1)} %get-tuple-element.99), channel_id=1, source_target_pairs={{0,4},{4,8},{8,12},{1,5},{5,9},{9,13},{2,6},{6,10},{10,14},{3,7},{... | collective-permute-start | bytes 15368 | tf_op jit(solution)/shard_map/ppermute | solution.py:44
  230.1 5.8 %collective-permute-start.18 = (f32[1,16,128]{2,1,0:T(8,128)S(1)}, f32[1,16,128]{2,1,0:T(8,128)S(1)}, u32[]{:S(2)}, u32[]{:S(2)}) collective-permute-start(f32[1,16,128]{2,1,0:T(8,128)S(1)} %slice.1129), channel_id=1, source_target_pairs={{16,0},{17,1},{18,2},{19,3},{20,4},{21,5},{22,6},{23,7},{24,8},{25... | collective-permute-start | bytes 24584 | tf_op jit(solution)/shard_map/ppermute | solution.py:46
  231.4 5.9 %collective-permute-start.19 = (f32[1,16,128]{2,1,0:T(8,128)S(1)}, f32[1,16,128]{2,1,0:T(8,128)S(1)}, u32[]{:S(2)}, u32[]{:S(2)}) collective-permute-start(f32[1,16,128]{2,1,0:T(8,128)S(1)} %slice.1129), channel_id=1, source_target_pairs={{0,16},{1,17},{2,18},{3,19},{4,20},{5,21},{6,22},{7,23},{8,24},{9,... | collective-permute-start | bytes 24584 | tf_op jit(solution)/shard_map/ppermute | solution.py:44
  237.3 7.7 %collective-permute-start.20 = (f32[10,1,128]{2,1,0:T(1,128)S(1)}, f32[10,1,128]{2,1,0:T(1,128)S(1)}, u32[]{:S(2)}, u32[]{:S(2)}) collective-permute-start(f32[10,1,128]{2,1,0:T(1,128)S(1)} %get-tuple-element.96), channel_id=1, source_target_pairs={{4,0},{8,4},{12,8},{5,1},{9,5},{13,9},{6,2},{10,6},{14,10},{7,3},{... | collective-permute-start | bytes 15368 | tf_op jit(solution)/shard_map/ppermute | solution.py:46
  238.6 6.4 %collective-permute-start.21 = (f32[10,1,128]{2,1,0:T(1,128)S(1)}, f32[10,1,128]{2,1,0:T(1,128)S(1)}, u32[]{:S(2)}, u32[]{:S(2)}) collective-permute-start(f32[10,1,128]{2,1,0:T(1,128)S(1)} %get-tuple-element.95), channel_id=1, source_target_pairs={{0,4},{4,8},{8,12},{1,5},{5,9},{9,13},{2,6},{6,10},{10,14},{3,7},{... | collective-permute-start | bytes 15368 | tf_op jit(solution)/shard_map/ppermute | solution.py:44
  250.9 5.9 %collective-permute-start.24 = (f32[1,16,128]{2,1,0:T(8,128)S(1)}, f32[1,16,128]{2,1,0:T(8,128)S(1)}, u32[]{:S(2)}, u32[]{:S(2)}) collective-permute-start(f32[1,16,128]{2,1,0:T(8,128)S(1)} %get-tuple-element.108), channel_id=1, source_target_pairs={{16,0},{17,1},{18,2},{19,3},{20,4},{21,5},{22,6},{23,7},{24,8},{25... | collective-permute-start | bytes 24584 | tf_op jit(solution)/shard_map/ppermute | solution.py:46
  252.2 5.9 %collective-permute-start.25 = (f32[1,16,128]{2,1,0:T(8,128)S(1)}, f32[1,16,128]{2,1,0:T(8,128)S(1)}, u32[]{:S(2)}, u32[]{:S(2)}) collective-permute-start(f32[1,16,128]{2,1,0:T(8,128)S(1)} %get-tuple-element.107), channel_id=1, source_target_pairs={{0,16},{1,17},{2,18},{3,19},{4,20},{5,21},{6,22},{7,23},{8,24},{9,... | collective-permute-start | bytes 24584 | tf_op jit(solution)/shard_map/ppermute | solution.py:44
  258.1 5.9 %collective-permute-start.26 = (f32[10,1,128]{2,1,0:T(1,128)S(1)}, f32[10,1,128]{2,1,0:T(1,128)S(1)}, u32[]{:S(2)}, u32[]{:S(2)}) collective-permute-start(f32[10,1,128]{2,1,0:T(1,128)S(1)} %get-tuple-element.92), channel_id=1, source_target_pairs={{4,0},{8,4},{12,8},{5,1},{9,5},{13,9},{6,2},{10,6},{14,10},{7,3},{... | collective-permute-start | bytes 15368 | tf_op jit(solution)/shard_map/ppermute | solution.py:46
  259.4 5.9 %collective-permute-start.27 = (f32[10,1,128]{2,1,0:T(1,128)S(1)}, f32[10,1,128]{2,1,0:T(1,128)S(1)}, u32[]{:S(2)}, u32[]{:S(2)}) collective-permute-start(f32[10,1,128]{2,1,0:T(1,128)S(1)} %get-tuple-element.91), channel_id=1, source_target_pairs={{0,4},{4,8},{8,12},{1,5},{5,9},{9,13},{2,6},{6,10},{10,14},{3,7},{... | collective-permute-start | bytes 15368 | tf_op jit(solution)/shard_map/ppermute | solution.py:44
  322.5 16.1 %collective-permute-start.36 = (f32[1,16,128]{2,1,0:T(8,128)S(1)}, f32[1,16,128]{2,1,0:T(8,128)S(1)}, u32[]{:S(2)}, u32[]{:S(2)}) collective-permute-start(f32[1,16,128]{2,1,0:T(8,128)S(1)} %slice.1200), channel_id=1, source_target_pairs={{16,0},{17,1},{18,2},{19,3},{20,4},{21,5},{22,6},{23,7},{24,8},{25... | collective-permute-start | bytes 24584 | tf_op jit(solution)/shard_map/ppermute | solution.py:46
  323.8 14.8 %collective-permute-start.37 = (f32[1,16,128]{2,1,0:T(8,128)S(1)}, f32[1,16,128]{2,1,0:T(8,128)S(1)}, u32[]{:S(2)}, u32[]{:S(2)}) collective-permute-start(f32[1,16,128]{2,1,0:T(8,128)S(1)} %slice.1200), channel_id=1, source_target_pairs={{0,16},{1,17},{2,18},{3,19},{4,20},{5,21},{6,22},{7,23},{8,24},{9,... | collective-permute-start | bytes 24584 | tf_op jit(solution)/shard_map/ppermute | solution.py:44
  332.8 11.8 %collective-permute-start.30 = (f32[1,16,128]{2,1,0:T(8,128)S(1)}, f32[1,16,128]{2,1,0:T(8,128)S(1)}, u32[]{:S(2)}, u32[]{:S(2)}) collective-permute-start(f32[1,16,128]{2,1,0:T(8,128)S(1)} %get-tuple-element.106), channel_id=1, source_target_pairs={{16,0},{17,1},{18,2},{19,3},{20,4},{21,5},{22,6},{23,7},{24,8},{25... | collective-permute-start | bytes 24584 | tf_op jit(solution)/shard_map/ppermute | solution.py:46
  334.1 10.5 %collective-permute-start.31 = (f32[1,16,128]{2,1,0:T(8,128)S(1)}, f32[1,16,128]{2,1,0:T(8,128)S(1)}, u32[]{:S(2)}, u32[]{:S(2)}) collective-permute-start(f32[1,16,128]{2,1,0:T(8,128)S(1)} %get-tuple-element.105), channel_id=1, source_target_pairs={{0,16},{1,17},{2,18},{3,19},{4,20},{5,21},{6,22},{7,23},{8,24},{9,... | collective-permute-start | bytes 24584 | tf_op jit(solution)/shard_map/ppermute | solution.py:44
  338.7 11.8 %collective-permute-start.38 = (f32[10,1,128]{2,1,0:T(1,128)S(1)}, f32[10,1,128]{2,1,0:T(1,128)S(1)}, u32[]{:S(2)}, u32[]{:S(2)}) collective-permute-start(f32[10,1,128]{2,1,0:T(1,128)S(1)} %get-tuple-element.84), channel_id=1, source_target_pairs={{4,0},{8,4},{12,8},{5,1},{9,5},{13,9},{6,2},{10,6},{14,10},{7,3},{... | collective-permute-start | bytes 15368 | tf_op jit(solution)/shard_map/ppermute | solution.py:46
  340.0 10.5 %collective-permute-start.39 = (f32[10,1,128]{2,1,0:T(1,128)S(1)}, f32[10,1,128]{2,1,0:T(1,128)S(1)}, u32[]{:S(2)}, u32[]{:S(2)}) collective-permute-start(f32[10,1,128]{2,1,0:T(1,128)S(1)} %get-tuple-element.83), channel_id=1, source_target_pairs={{0,4},{4,8},{8,12},{1,5},{5,9},{9,13},{2,6},{6,10},{10,14},{3,7},{... | collective-permute-start | bytes 15368 | tf_op jit(solution)/shard_map/ppermute | solution.py:44
  344.6 10.3 %collective-permute-start.32 = (f32[10,1,128]{2,1,0:T(1,128)S(1)}, f32[10,1,128]{2,1,0:T(1,128)S(1)}, u32[]{:S(2)}, u32[]{:S(2)}) collective-permute-start(f32[10,1,128]{2,1,0:T(1,128)S(1)} %get-tuple-element.88), channel_id=1, source_target_pairs={{4,0},{8,4},{12,8},{5,1},{9,5},{13,9},{6,2},{10,6},{14,10},{7,3},{... | collective-permute-start | bytes 15368 | tf_op jit(solution)/shard_map/ppermute | solution.py:46
  345.9 9.1 %collective-permute-start.33 = (f32[10,1,128]{2,1,0:T(1,128)S(1)}, f32[10,1,128]{2,1,0:T(1,128)S(1)}, u32[]{:S(2)}, u32[]{:S(2)}) collective-permute-start(f32[10,1,128]{2,1,0:T(1,128)S(1)} %get-tuple-element.87), channel_id=1, source_target_pairs={{0,4},{4,8},{8,12},{1,5},{5,9},{9,13},{2,6},{6,10},{10,14},{3,7},{... | collective-permute-start | bytes 15368 | tf_op jit(solution)/shard_map/ppermute | solution.py:44
  350.6 54.2 %collective-permute-start.40 = (f32[10,18,1]{2,1,0:T(8,128)S(1)}, f32[10,18,1]{2,1,0:T(8,128)S(1)}, u32[]{:S(2)}, u32[]{:S(2)}) collective-permute-start(f32[10,18,1]{2,1,0:T(8,128)S(1)} %get-tuple-element.58), channel_id=1, source_target_pairs={{1,0},{2,1},{3,2},{5,4},{6,5},{7,6},{9,8},{10,9},{11,10},{13,12},{... | collective-permute-start | bytes 2168 | tf_op jit(solution)/shard_map/ppermute | solution.py:46
  351.9 52.9 %collective-permute-start.41 = (f32[10,18,1]{2,1,0:T(8,128)S(1)}, f32[10,18,1]{2,1,0:T(8,128)S(1)}, u32[]{:S(2)}, u32[]{:S(2)}) collective-permute-start(f32[10,18,1]{2,1,0:T(8,128)S(1)} %get-tuple-element.57), channel_id=1, source_target_pairs={{0,1},{1,2},{2,3},{4,5},{5,6},{6,7},{8,9},{9,10},{10,11},{12,13},{... | collective-permute-start | bytes 2168 | tf_op jit(solution)/shard_map/ppermute | solution.py:44
  355.1 6.0 %collective-permute-start.34 = (f32[10,18,1]{2,1,0:T(8,128)S(1)}, f32[10,18,1]{2,1,0:T(8,128)S(1)}, u32[]{:S(2)}, u32[]{:S(2)}) collective-permute-start(f32[10,18,1]{2,1,0:T(8,128)S(1)} %get-tuple-element.60), channel_id=1, source_target_pairs={{1,0},{2,1},{3,2},{5,4},{6,5},{7,6},{9,8},{10,9},{11,10},{13,12},{... | collective-permute-start | bytes 2168 | tf_op jit(solution)/shard_map/ppermute | solution.py:46
  (12 other events, 65.1 us)
